TPU v7x, 32 devices: a whole 2x2x4 slice. The times are simulated.
32 devices in a mesh: gx: 8 (over z, x), yz: 4 (over y, core).
Axes of the slice: x: 2, y: 2, z: 4, core: 2. Of those that a mesh axis runs over, the one named last changes fastest.
Arguments:
- state: float32 [4, 256, 192, 256], P(None, 'gx', 'yz'), may hold values from -6 to 6
- mean_flow: float32 [256, 192, 256], P('gx', 'yz'), may hold values from 0.2 to 1.2
- face_cell: int32 [6144], P(('gx', 'yz')), may hold values from 0 to 12582911, as said below
- face_normal: float32 [3, 6144], P(None, ('gx', 'yz')), may hold values from -3 to 3
- face_pos: float32 [3, 6144], P(None, ('gx', 'yz')), may hold values from -2 to 2
- observer_pos: float32 [3, 512], replicated, may hold values from 4 to 12
- time_bin: int32 [6144, 512], P(('gx', 'yz')), may hold values from 0 to 63
Outputs:
- state_next: float32 [4, 256, 192, 256], P(None, 'gx', 'yz')
- signal: float32 [512, 64], P(('gx', 'yz'))
Inputs may be any that keep to these rules, and one draw needn't show every extreme that they name: `face_cell`: face j is held by device j // 192 of gx+yz, and its cell, numbered (x 192 + y) * 256 + z, lies in that device's block of grid cells.
All inputs are finite; a program needn't handle non-finite values.
Results may differ from a plain program's by a relative error of at most 0.000084.
Values sent between devices are 32-bit elements; how exact they have to be, the bound alone decides.
A program may use at most 192 MiB of HBM per device.

v0:
```python
import jax
import jax.numpy as jnp
from jax import lax
from jax.sharding import PartitionSpec as P

BINS = 64
time_step = 0.25
four_pi = 4.0 * 3.141592653589793
highest = lax.Precision.HIGHEST


def extended(block, sides, width):
    for axis, dim in sides:
        count = lax.axis_size(axis)
        forward = [(i, i + 1) for i in range(count - 1)]
        backward = [(target, source) for source, target in forward]
        low = lax.ppermute(
            lax.slice_in_dim(block, block.shape[dim] - width, None, axis=dim), axis, forward
        )
        high = lax.ppermute(lax.slice_in_dim(block, 0, width, axis=dim), axis, backward)
        block = jnp.concatenate([low, block, high], axis=dim)
    return block


def diagonals(count):
    index = jnp.arange(count)
    third = jnp.full((count,), 1.0 / 3.0, jnp.float32)
    quarter = jnp.float32(0.25)
    lower = jnp.where(index == 1, quarter, third)
    lower = jnp.where(index == count - 2, quarter, lower)
    lower = jnp.where(index == count - 1, jnp.float32(2.0), lower)
    lower = jnp.where(index == 0, jnp.float32(0.0), lower)
    upper = jnp.where(index == 1, quarter, third)
    upper = jnp.where(index == count - 2, quarter, upper)
    upper = jnp.where(index == 0, jnp.float32(2.0), upper)
    upper = jnp.where(index == count - 1, jnp.float32(0.0), upper)
    return (lower, jnp.ones((count,), jnp.float32), upper)


def inverse_of(lower, middle, upper):
    count = middle.shape[0]
    return lax.linalg.tridiagonal_solve(lower, middle, upper, jnp.eye(count, dtype=jnp.float32))


def compact_rhs(field, axis):
    count = field.shape[axis]
    widths = [(2, 2) if dimension == axis else (0, 0) for dimension in range(field.ndim)]
    padded = jnp.pad(field, widths)

    def take(first, last):
        return lax.slice_in_dim(padded, first, last, axis=axis)

    def plane(index):
        return lax.slice_in_dim(field, index, index + 1, axis=axis)

    inner = 7.0 / 9.0 * (take(3, count + 3) - take(1, count + 1)) + 1.0 / 36.0 * (
        take(4, count + 4) - take(0, count)
    )
    first_row = 0.5 * (4.0 * plane(1) + plane(2) - 5.0 * plane(0))
    second_row = 0.75 * (plane(2) - plane(0))
    before_last = 0.75 * (plane(count - 1) - plane(count - 3))
    last_row = 0.5 * (5.0 * plane(count - 1) - 4.0 * plane(count - 2) - plane(count - 3))
    middle_rows = lax.slice_in_dim(inner, 2, count - 2, axis=axis)
    return jnp.concatenate([first_row, second_row, middle_rows, before_last, last_row], axis)


def explicit_y(padded, count):

    def take(shift):
        return lax.slice_in_dim(padded, 3 + shift, 3 + shift + count, axis=2)

    return (
        0.75 * (take(1) - take(-1))
        - 0.15 * (take(2) - take(-2))
        + 1.0 / 60.0 * (take(3) - take(-3))
    )


def transposed_x(fields):
    part = lax.all_to_all(fields, "gx", split_axis=2, concat_axis=1, tiled=True)
    inverse = inverse_of(*diagonals(part.shape[1]))
    rhs = compact_rhs(part, 1)
    solved = jnp.einsum("ij,fjab->fiab", inverse, rhs, precision=highest)
    return lax.all_to_all(solved, "gx", split_axis=1, concat_axis=2, tiled=True)


def per_device(state, mean_flow, face_cell, face_normal, face_pos, observer_pos, time_bin):
    cells, width, depth = (state.shape[1], state.shape[2], state.shape[3])
    fields = jnp.concatenate([state, mean_flow[None]], 0)
    x_rates = transposed_x(fields)
    crossing = extended(fields[0::2], (("yz", 2),), 3)
    y_rates = explicit_y(crossing, width)
    z_fields = jnp.concatenate([fields[0:1], fields[3:5]], 0)
    z_inverse = inverse_of(*diagonals(depth))
    z_rates = jnp.dot(compact_rhs(z_fields, 3), z_inverse.T, precision=highest)
    pressure, stream, lateral, vertical = (state[0], state[1], state[2], state[3])
    pressure_rate = -(mean_flow * x_rates[0] + x_rates[1] + y_rates[1] + z_rates[1])
    stream_rate = -(
        mean_flow * x_rates[1]
        + stream * x_rates[4]
        + lateral * y_rates[2]
        + vertical * z_rates[2]
        + x_rates[0]
    )
    lateral_rate = -(mean_flow * x_rates[2] + y_rates[0])
    vertical_rate = -(mean_flow * x_rates[3] + z_rates[0])
    rates = jnp.stack([pressure_rate, stream_rate, lateral_rate, vertical_rate])
    state_next = state + time_step * rates
    planes = width * lax.axis_size("yz")
    block = lax.axis_index("gx")
    group = lax.axis_index("yz")
    along_x = face_cell // (planes * depth) - block * cells
    along_y = face_cell // depth % planes - group * width
    along_z = face_cell % depth
    local_cell = (along_x * width + along_y) * depth + along_z
    face_rates = rates.reshape(4, -1)[:, local_cell]
    face_pressure = state_next[0].reshape(-1)[local_cell]
    normal_rate = (
        face_normal[0] * face_rates[1]
        + face_normal[1] * face_rates[2]
        + face_normal[2] * face_rates[3]
    )
    offset_x = observer_pos[0][None, :] - face_pos[0][:, None]
    offset_y = observer_pos[1][None, :] - face_pos[1][:, None]
    offset_z = observer_pos[2][None, :] - face_pos[2][:, None]
    distance = jnp.sqrt(offset_x * offset_x + offset_y * offset_y + offset_z * offset_z)
    normal_r = (
        face_normal[0][:, None] * offset_x
        + face_normal[1][:, None] * offset_y
        + face_normal[2][:, None] * offset_z
    ) / distance
    contribution = (
        normal_rate[:, None]
        + (face_rates[0][:, None] + face_pressure[:, None] / distance) * normal_r
    ) / (four_pi * distance)
    onehot = (time_bin[:, :, None] == jnp.arange(BINS, dtype=jnp.int32)).astype(jnp.float32)
    signal = lax.psum_scatter(
        jnp.sum(contribution[:, :, None] * onehot, axis=0),
        ("gx", "yz"),
        scatter_dimension=0,
        tiled=True,
    )
    return (state_next, signal)


def solution(mesh):
    in_specs = (
        P(None, "gx", "yz", None),
        P("gx", "yz", None),
        P(("gx", "yz")),
        P(None, ("gx", "yz")),
        P(None, ("gx", "yz")),
        P(),
        P(("gx", "yz"), None),
    )
    out_specs = (P(None, "gx", "yz", None), P(("gx", "yz"), None))
    return jax.shard_map(
        per_device, mesh=mesh, in_specs=in_specs, out_specs=out_specs, check_vma=False
    )
```

profile of v0, /device:TPU:0, one launch (start us, length us, event | category | flops | bytes accessed | tf_op | source)
XLA Modules:
  0.0 1276.9 jit_solution(14212559706522243462)
XLA Ops:
  31.2 458.7 %while.8 = (s32[]{:T(128)}, f32[]{:T(128)}, f32[256]{0:T(256)S(1)}, f32[7,32]{1,0:T(8,128)S(1)}, f32[7,32,256]{2,1,0:T(8,128)S(1)}, /*index=5*/f32[7,32]{1,0:T(8...) while((s32[]{:T(128)}, f32[]{:T(128)}, ...), condition=%wide.region_1.2_spmd, body=%wide.region_0.1_spmd.sunk | while | flops 24705 | bytes 269033 | solution.py:42
  74.5 20.3 %subtract_divide_fusion.125 = (f32[256]{0:T(256)S(1)}, f32[256]{0:T(256)S(1)}, f32[256]{0:T(256)S(1)}, f32[256]{0:T(256)S(1)}, f32[256]{0:T(256)S(1)}, /*index=5...) fusion(f32[256]{0:T(256)S(1)} %bitcast.1217, ...), kind=kLoop, calls=%fused_computation.37.clone.1 | loop fusion | flops 24576 | bytes 66816 | tf_op jit(solution)/shard_map/while/body/eval_jaxpr/div | solution.py:42
  140.0 20.3 %subtract_divide_fusion.125 = (f32[256]{0:T(256)S(1)}, f32[256]{0:T(256)S(1)}, f32[256]{0:T(256)S(1)}, f32[256]{0:T(256)S(1)}, f32[256]{0:T(256)S(1)}, /*index=5...) fusion(f32[256]{0:T(256)S(1)} %bitcast.1217, ...), kind=kLoop, calls=%fused_computation.37.clone.1 | loop fusion | flops 24576 | bytes 66816 | tf_op jit(solution)/shard_map/while/body/eval_jaxpr/div | solution.py:42
  205.5 20.3 %subtract_divide_fusion.125 = (f32[256]{0:T(256)S(1)}, f32[256]{0:T(256)S(1)}, f32[256]{0:T(256)S(1)}, f32[256]{0:T(256)S(1)}, f32[256]{0:T(256)S(1)}, /*index=5...) fusion(f32[256]{0:T(256)S(1)} %bitcast.1217, ...), kind=kLoop, calls=%fused_computation.37.clone.1 | loop fusion | flops 24576 | bytes 66816 | tf_op jit(solution)/shard_map/while/body/eval_jaxpr/div | solution.py:42
  271.0 20.3 %subtract_divide_fusion.125 = (f32[256]{0:T(256)S(1)}, f32[256]{0:T(256)S(1)}, f32[256]{0:T(256)S(1)}, f32[256]{0:T(256)S(1)}, f32[256]{0:T(256)S(1)}, /*index=5...) fusion(f32[256]{0:T(256)S(1)} %bitcast.1217, ...), kind=kLoop, calls=%fused_computation.37.clone.1 | loop fusion | flops 24576 | bytes 66816 | tf_op jit(solution)/shard_map/while/body/eval_jaxpr/div | solution.py:42
  336.6 20.3 %subtract_divide_fusion.125 = (f32[256]{0:T(256)S(1)}, f32[256]{0:T(256)S(1)}, f32[256]{0:T(256)S(1)}, f32[256]{0:T(256)S(1)}, f32[256]{0:T(256)S(1)}, /*index=5...) fusion(f32[256]{0:T(256)S(1)} %bitcast.1217, ...), kind=kLoop, calls=%fused_computation.37.clone.1 | loop fusion | flops 24576 | bytes 66816 | tf_op jit(solution)/shard_map/while/body/eval_jaxpr/div | solution.py:42
  402.1 20.3 %subtract_divide_fusion.125 = (f32[256]{0:T(256)S(1)}, f32[256]{0:T(256)S(1)}, f32[256]{0:T(256)S(1)}, f32[256]{0:T(256)S(1)}, f32[256]{0:T(256)S(1)}, /*index=5...) fusion(f32[256]{0:T(256)S(1)} %bitcast.1217, ...), kind=kLoop, calls=%fused_computation.37.clone.1 | loop fusion | flops 24576 | bytes 66816 | tf_op jit(solution)/shard_map/while/body/eval_jaxpr/div | solution.py:42
  467.6 20.3 %subtract_divide_fusion.125 = (f32[256]{0:T(256)S(1)}, f32[256]{0:T(256)S(1)}, f32[256]{0:T(256)S(1)}, f32[256]{0:T(256)S(1)}, f32[256]{0:T(256)S(1)}, /*index=5...) fusion(f32[256]{0:T(256)S(1)} %bitcast.1217, ...), kind=kLoop, calls=%fused_computation.37.clone.1 | loop fusion | flops 24576 | bytes 66816 | tf_op jit(solution)/shard_map/while/body/eval_jaxpr/div | solution.py:42
  529.7 19.0 %subtract_divide_fusion.32 = (f32[256]{0:T(256)S(1)}, f32[256]{0:T(256)S(1)}, f32[256]{0:T(256)S(1)}, f32[256]{0:T(256)S(1)}, f32[256]{0:T(256)S(1)}, /*index=5*...) fusion(f32[256]{0:T(256)S(1)} %bitcast.1418, ...), kind=kLoop, calls=%fused_computation.305 | loop fusion | flops 23808 | bytes 64760 | tf_op jit(solution)/shard_map/eval_jaxpr/div | solution.py:42
  551.3 151.0 %while.9 = (s32[]{:T(128)}, f32[256]{0:T(256)S(1)}, f32[7,32,256]{2,1,0:T(8,128)S(1)}, f32[7,32,256]{2,1,0:T(8,128)S(1)}, f32[7,32]{1,0:T(8,128)S(1)}, /*index=5...) while((s32[]{:T(128)}, f32[256]{0:T(256)S(1)}, ...), condition=%wide.region_3.4_spmd, body=%wide.region_2.3_spmd.sunk | while | flops 16418 | bytes 266713 | solution.py:42
  553.0 19.7 %multiply_subtract_fusion.125 = (f32[256]{0:T(256)S(1)}, f32[256]{0:T(256)S(1)}, f32[256]{0:T(256)S(1)}, f32[256]{0:T(256)S(1)}, f32[256]{0:T(256)S(1)}, /*index...) fusion(f32[256]{0:T(256)S(1)} %bitcast.1266, ...), kind=kLoop, calls=%fused_computation.103.clone.1 | loop fusion | flops 16384 | bytes 66688 | tf_op jit(solution)/shard_map/while/body/eval_jaxpr/sub | solution.py:42
  574.6 19.7 %multiply_subtract_fusion.125 = (f32[256]{0:T(256)S(1)}, f32[256]{0:T(256)S(1)}, f32[256]{0:T(256)S(1)}, f32[256]{0:T(256)S(1)}, f32[256]{0:T(256)S(1)}, /*index...) fusion(f32[256]{0:T(256)S(1)} %bitcast.1266, ...), kind=kLoop, calls=%fused_computation.103.clone.1 | loop fusion | flops 16384 | bytes 66688 | tf_op jit(solution)/shard_map/while/body/eval_jaxpr/sub | solution.py:42
  596.1 19.7 %multiply_subtract_fusion.125 = (f32[256]{0:T(256)S(1)}, f32[256]{0:T(256)S(1)}, f32[256]{0:T(256)S(1)}, f32[256]{0:T(256)S(1)}, f32[256]{0:T(256)S(1)}, /*index...) fusion(f32[256]{0:T(256)S(1)} %bitcast.1266, ...), kind=kLoop, calls=%fused_computation.103.clone.1 | loop fusion | flops 16384 | bytes 66688 | tf_op jit(solution)/shard_map/while/body/eval_jaxpr/sub | solution.py:42
  617.7 19.7 %multiply_subtract_fusion.125 = (f32[256]{0:T(256)S(1)}, f32[256]{0:T(256)S(1)}, f32[256]{0:T(256)S(1)}, f32[256]{0:T(256)S(1)}, f32[256]{0:T(256)S(1)}, /*index...) fusion(f32[256]{0:T(256)S(1)} %bitcast.1266, ...), kind=kLoop, calls=%fused_computation.103.clone.1 | loop fusion | flops 16384 | bytes 66688 | tf_op jit(solution)/shard_map/while/body/eval_jaxpr/sub | solution.py:42
  639.2 19.7 %multiply_subtract_fusion.125 = (f32[256]{0:T(256)S(1)}, f32[256]{0:T(256)S(1)}, f32[256]{0:T(256)S(1)}, f32[256]{0:T(256)S(1)}, f32[256]{0:T(256)S(1)}, /*index...) fusion(f32[256]{0:T(256)S(1)} %bitcast.1266, ...), kind=kLoop, calls=%fused_computation.103.clone.1 | loop fusion | flops 16384 | bytes 66688 | tf_op jit(solution)/shard_map/while/body/eval_jaxpr/sub | solution.py:42
  660.8 19.7 %multiply_subtract_fusion.125 = (f32[256]{0:T(256)S(1)}, f32[256]{0:T(256)S(1)}, f32[256]{0:T(256)S(1)}, f32[256]{0:T(256)S(1)}, f32[256]{0:T(256)S(1)}, /*index...) fusion(f32[256]{0:T(256)S(1)} %bitcast.1266, ...), kind=kLoop, calls=%fused_computation.103.clone.1 | loop fusion | flops 16384 | bytes 66688 | tf_op jit(solution)/shard_map/while/body/eval_jaxpr/sub | solution.py:42
  682.4 19.7 %multiply_subtract_fusion.125 = (f32[256]{0:T(256)S(1)}, f32[256]{0:T(256)S(1)}, f32[256]{0:T(256)S(1)}, f32[256]{0:T(256)S(1)}, f32[256]{0:T(256)S(1)}, /*index...) fusion(f32[256]{0:T(256)S(1)} %bitcast.1266, ...), kind=kLoop, calls=%fused_computation.103.clone.1 | loop fusion | flops 16384 | bytes 66688 | tf_op jit(solution)/shard_map/while/body/eval_jaxpr/sub | solution.py:42
  702.3 19.1 %multiply_subtract_fusion.32 = (f32[256]{0:T(256)S(1)}, f32[256]{0:T(256)S(1)}, f32[256]{0:T(256)S(1)}, f32[256]{0:T(256)S(1)}, f32[256]{0:T(256)S(1)}, /*index=...) fusion(f32[256]{0:T(256)S(1)} %bitcast.1364, ...), kind=kLoop, calls=%fused_computation.274 | loop fusion | flops 15872 | bytes 64636 | tf_op jit(solution)/shard_map/eval_jaxpr/sub | solution.py:42
  740.1 25.2 %pad_slice_fusion.3 = (f32[5,256,6,256]{1,3,2,0:T(8,128)}, f32[5,256,6,256]{1,3,2,0:T(8,128)}, f32[5,256,6,256]{1,3,2,0:T(8,128)}, f32[5,256,6,256]{1,3,2,0:T(8,128)}) fusion(f32[5,256,6,256]{1,3,2,0:T(8,128)} %copy.197), kind=kLoop, calls=%fused_computation.140 | loop fusion | bytes 39321600 | tf_op jit(solution)/shard_map/slice | solution.py:51
  775.4 16.3 %fusion.1 = f32[5,252,6,256]{1,3,2,0:T(8,128)} fusion(f32[5,256,6,256]{1,3,2,0:T(8,128)} %get-tuple-element.521, f32[5,256,6,256]{1,3,2,0:T(8,128)} %get-tuple-element.520, f32[5,256,6,256]{1,3,2,0:T(8,128)} %get-tuple-element.519, f32[5,256,6,256]{1,3,2,0:T(8,128)} %get-tuple-element.518), kind=kLoop, calls=%fused_computation.157 | loop fusion | flops 9676800 | bytes 38707200 | tf_op jit(solution)/shard_map/add | solution.py:56
  791.7 17.8 %concatenate.55 = f32[5,256,6,256]{1,3,2,0:T(8,128)} concatenate(f32[5,1,6,256]{1,3,2,0:T(8,128)} %copy.198, f32[5,1,6,256]{1,3,2,0:T(8,128)} %copy.199, f32[5,252,6,256]{1,3,2,0:T(8,128)} %fusion.1, f32[5,1,6,256]{1,3,2,0:T(8,128)} %copy.200, f32[5,1,6,256]{1,3,2,0:T(8,128)} %copy.201), dimensions={1} | concatenate | bytes 15728640 | tf_op jit(solution)/shard_map/concatenate | solution.py:64
  960.2 35.8 %fusion.8 = f32[3,32,48,256]{3,2,1,0:T(8,128)} fusion(f32[3,32,48,256]{3,1,2,0:T(8,128)} %get-tuple-element.529, f32[3,32,48,256]{3,1,2,0:T(8,128)} %get-tuple-element.526, f32[3,32,48,256]{3,1,2,0:T(8,128)} %get-tuple-element.528, f32[3,32,48,256]{3,1,2,0:T(8,128)} %get-tuple-element.525, f32[3,32,48,256]{3,1,2,0:T(8,128)} %get-tuple-element.527, ...), kind=kLoop, calls=%fused_computation.176 | loop fusion | flops 9437184 | bytes 33030144 | tf_op jit(solution)/shard_map/add | solution.py:73
  996.0 67.9 %all-to-all-done.1 = f32[5,256,6,256]{3,2,0,1:T(8,128)} async-done(((f32[5,256,6,256]{3,2,0,1:T(8,128)}), f32[5,256,6,256]{3,2,0,1:T(8,128)}, u32[]{:S(2)}, u32[]{:S(2)}) %all-to-all-start.1) | async-done | bytes 7864352 | tf_op jit(solution)/shard_map/all_to_all | solution.py:84
  1135.0 134.8 %reduce-scatter.4.cloned.1.call-done = f32[16,64]{1,0:T(8,128)} async-done(((f32[512,64]{1,0:T(8,128)}), f32[16,64]{1,0:T(8,128)}) %reduce-scatter.4.cloned.1.call-update) | async-done | bytes 4112
  (290 shorter events, 318.7 us)
Async XLA Ops:
  11.1 3.1 copy-start
  21.8 699.7 %all-to-all-start = ((f32[5,32,48,256]{3,1,0,2:T(8,128)}), f32[5,32,48,256]{3,1,0,2:T(8,128)}, u32[]{:S(2)}, u32[]{:S(2)}) async-start(f32[5,32,48,256]{3,1,0,2:T(8,128)} %copy.194), calls=%async_computation | async-start | bytes 15728640 | tf_op jit(solution)/shard_map/all_to_all | solution.py:80
  830.4 233.5 %all-to-all-start.1 = ((f32[5,256,6,256]{3,2,0,1:T(8,128)}), f32[5,256,6,256]{3,2,0,1:T(8,128)}, u32[]{:S(2)}, u32[]{:S(2)}) async-start(f32[5,256,6,256]{3,2,0,1:T(8,128)} %copy.202), calls=%async_computation.1 | async-start | bytes 20971520 | tf_op jit(solution)/shard_map/all_to_all | solution.py:84
  836.4 433.4 %reduce-scatter.4.cloned.1.call-start = ((), (), s32[]{:S(2)}) async-start(), calls=%async_computation.3 | async-start | bytes 270336
  839.1 6.7 copy-start.1
  839.1 6.7 copy-start.3
  840.1 85.1 %collective-permute-start.1 = (f32[3,32,3,256]{3,1,2,0:T(8,128)}, f32[3,32,3,256]{3,1,2,0:T(8,128)}, u32[]{:S(2)}, u32[]{:S(2)}) collective-permute-start(f32[3,32,3,256]{3,1,2,0:T(8,128)} %copy.285), channel_id=1, source_target_pairs={{0,1},{1,2},{2,3},{4,5},{5,6},{6,7},{8,9},{9,10},{10,11},{12,13},{... | collective-permute-start | bytes 884744 | tf_op jit(solution)/shard_map/ppermute | solution.py:17
  843.0 92.7 %collective-permute-start = (f32[3,32,3,256]{3,1,2,0:T(8,128)}, f32[3,32,3,256]{3,1,2,0:T(8,128)}, u32[]{:S(2)}, u32[]{:S(2)}) collective-permute-start(f32[3,32,3,256]{3,1,2,0:T(8,128)} %copy.286), channel_id=1, source_target_pairs={{1,0},{2,1},{3,2},{5,4},{6,5},{7,6},{9,8},{10,9},{11,10},{13,12},{... | collective-permute-start | bytes 884744 | tf_op jit(solution)/shard_map/ppermute | solution.py:20
  904.1 11.4 copy-start.14
  904.1 11.5 copy-start.12
  904.1 11.5 copy-start.13
  916.2 8.3 copy-start.8
  1063.9 11.3 slice-start.4
  1070.5 4.7 slice-start.2
  1070.5 4.7 slice-start.5
  1071.9 3.3 slice-start
  1071.9 4.6 slice-start.3
  1072.3 4.9 slice-start.1
  1072.3 5.3 copy-start.4
  1120.9 2.7 copy-start.5
  1123.6 2.6 copy-start.9
  1123.6 2.6 copy-start.10
  1123.6 2.7 copy-start.11
  1123.6 3.1 copy-start.6
  (2 other events, 4.8 us)
Sparse Core Ops, SparseCore 0:
  1135.1 134.6 reduce-scatter.3
where the time goes:
time: 1290 us; the launch traced here: 1280 us
  other arithmetic  432 us (33%)
  loops' own time  289 us (22%)
  local copies, waits for them, and re-layouts  264 us (20%)
  waiting for transfers between devices  203 us (16%)
  between operations  53.1 us (4%)
  matrix products  18.8 us (1%)
  starting transfers between devices  17 us (1%)
    another operation x2, loops' own time, inverse_of(): lax.linalg.tridiagonal_solve(lower, middle, upper, jnp.eye(count, dtype=j...  289 us
    div x8, other arithmetic, inverse_of(): lax.linalg.tridiagonal_solve(lower, middle, upper, jnp.eye(count, dtype=j...  161 us
    sub x8, other arithmetic, inverse_of(): lax.linalg.tridiagonal_solve(lower, middle, upper, jnp.eye(count, dtype=j...  157 us
    unnamed x2, waiting for transfers between devices  135 us
    all_to_all x1, waiting for transfers between devices, transposed_x(): return lax.all_to_all(solved, 'gx', split_axis=1, concat_axis=2, tiled=True)  67.9 us
    unnamed x54, local copies, waits for them, and re-layouts  38.1 us
    slice x85, local copies, waits for them, and re-layouts, inverse_of(): lax.linalg.tridiagonal_solve(lower, middle, upper, jnp.eye(count, dtype=j...  37.6 us
    add x1, other arithmetic, explicit_y(): 0.75 * (take(1) - take(-1)) - 0.15 * (take(2) - take(-2))  35.8 us
  transfers between devices with their start and end apart: 5, of which 2 were waited for; matrix products, arithmetic and copies ran while one was open for 41% of the time, Pallas kernels for 0%

commit v1 on v0

--- a/solution.py
+++ b/solution.py
@@ -81,7 +81,10 @@
     inverse = inverse_of(*diagonals(part.shape[1]))
     rhs = compact_rhs(part, 1)
     solved = jnp.einsum("ij,fjab->fiab", inverse, rhs, precision=highest)
-    return lax.all_to_all(solved, "gx", split_axis=1, concat_axis=2, tiled=True)
+    return jnp.concatenate(
+        lax.all_to_all(jnp.stack(jnp.split(solved, lax.axis_size("gx"), axis=1)), "gx", 0, 0),
+        axis=2,
+    )
 
 
 def per_device(state, mean_flow, face_cell, face_normal, face_pos, observer_pos, time_bin):

time: 1290 us -> 1190 us (0.922)
  waiting for transfers between devices: 203 us -> 147 us
  local copies, waits for them, and re-layouts: 264 us -> 222 us
    all_to_all x1, waiting for transfers between devices: 67.9 us -> 11.7 us  [transposed_x(): lax.all_to_all(jnp.stack(jnp.split(solved, lax.axis_size('gx'), axis=1)),...]
    slice x2, local copies, waits for them, and re-layouts: 33.4 us -> 19.9 us  [take(): return lax.slice_in_dim(padded, first, last, axis=axis)]
    all_to_all x2 -> x1, local copies, waits for them, and re-layouts: 16.9 us -> 4.01 us  [transposed_x(): part = lax.all_to_all(fields, 'gx', split_axis=2, concat_axis=1, tiled=True)]
    unnamed x54 -> x47, local copies, waits for them, and re-layouts: 38.1 us -> 45 us
  transfers between devices with their start and end apart: 5 -> 5, of which waited for: 2 -> 2; matrix products, arithmetic and copies ran while one was open for 41% -> 44% of each run, Pallas kernels for 0% -> 0%
where the time goes in v1:
time: 1190 us; the launch traced here: 1170 us
  other arithmetic  429 us (36%)
  loops' own time  285 us (24%)
  local copies, waits for them, and re-layouts  222 us (19%)
  waiting for transfers between devices  147 us (12%)
  between operations  53.4 us (4%)
  matrix products  18.5 us (2%)
  starting transfers between devices  16.9 us (1%)
    another operation x2, loops' own time, inverse_of(): lax.linalg.tridiagonal_solve(lower, middle, upper, jnp.eye(count, dtype=j...  285 us
    sub x8, other arithmetic, inverse_of(): lax.linalg.tridiagonal_solve(lower, middle, upper, jnp.eye(count, dtype=j...  159 us
    div x8, other arithmetic, inverse_of(): lax.linalg.tridiagonal_solve(lower, middle, upper, jnp.eye(count, dtype=j...  157 us
    unnamed x2, waiting for transfers between devices  135 us
    unnamed x47, local copies, waits for them, and re-layouts  45 us
    slice x85, local copies, waits for them, and re-layouts, inverse_of(): lax.linalg.tridiagonal_solve(lower, middle, upper, jnp.eye(count, dtype=j...  37.5 us
    concatenate x2, local copies, waits for them, and re-layouts, compact_rhs(): jnp.concatenate([first_row, second_row, middle_rows, before_last, last_ro...  36.3 us
    add x1, other arithmetic, explicit_y(): 0.75 * (take(1) - take(-1)) - 0.15 * (take(2) - take(-2))  35.8 us
  transfers between devices with their start and end apart: 5, of which 2 were waited for; matrix products, arithmetic and copies ran while one was open for 44% of the time, Pallas kernels for 0%

profile of v1, /device:TPU:0, one launch (start us, length us, event | category | flops | bytes accessed | tf_op | source)
XLA Modules:
  0.0 1172.3 jit_solution(3135238520413668037)
XLA Ops:
  30.5 446.5 %while.8 = (s32[]{:T(128)}, f32[]{:T(128)}, f32[256]{0:T(256)S(1)}, f32[7,32]{1,0:T(8,128)S(1)}, f32[7,32,256]{2,1,0:T(8,128)S(1)}, /*index=5*/f32[7,32]{1,0:T(8...) while((s32[]{:T(128)}, f32[]{:T(128)}, ...), condition=%wide.region_1.2_spmd, body=%wide.region_0.1_spmd.sunk | while | flops 24705 | bytes 269049 | solution.py:42
  73.8 19.7 %subtract_divide_fusion.125 = (f32[256]{0:T(256)S(1)}, f32[256]{0:T(256)S(1)}, f32[256]{0:T(256)S(1)}, f32[256]{0:T(256)S(1)}, f32[256]{0:T(256)S(1)}, /*index=5...) fusion(f32[256]{0:T(256)S(1)} %bitcast.1222, ...), kind=kLoop, calls=%fused_computation.37.clone.1 | loop fusion | flops 24576 | bytes 66816 | tf_op jit(solution)/shard_map/while/body/eval_jaxpr/div | solution.py:42
  137.6 19.7 %subtract_divide_fusion.125 = (f32[256]{0:T(256)S(1)}, f32[256]{0:T(256)S(1)}, f32[256]{0:T(256)S(1)}, f32[256]{0:T(256)S(1)}, f32[256]{0:T(256)S(1)}, /*index=5...) fusion(f32[256]{0:T(256)S(1)} %bitcast.1222, ...), kind=kLoop, calls=%fused_computation.37.clone.1 | loop fusion | flops 24576 | bytes 66816 | tf_op jit(solution)/shard_map/while/body/eval_jaxpr/div | solution.py:42
  201.4 19.7 %subtract_divide_fusion.125 = (f32[256]{0:T(256)S(1)}, f32[256]{0:T(256)S(1)}, f32[256]{0:T(256)S(1)}, f32[256]{0:T(256)S(1)}, f32[256]{0:T(256)S(1)}, /*index=5...) fusion(f32[256]{0:T(256)S(1)} %bitcast.1222, ...), kind=kLoop, calls=%fused_computation.37.clone.1 | loop fusion | flops 24576 | bytes 66816 | tf_op jit(solution)/shard_map/while/body/eval_jaxpr/div | solution.py:42
  265.1 19.7 %subtract_divide_fusion.125 = (f32[256]{0:T(256)S(1)}, f32[256]{0:T(256)S(1)}, f32[256]{0:T(256)S(1)}, f32[256]{0:T(256)S(1)}, f32[256]{0:T(256)S(1)}, /*index=5...) fusion(f32[256]{0:T(256)S(1)} %bitcast.1222, ...), kind=kLoop, calls=%fused_computation.37.clone.1 | loop fusion | flops 24576 | bytes 66816 | tf_op jit(solution)/shard_map/while/body/eval_jaxpr/div | solution.py:42
  328.9 19.7 %subtract_divide_fusion.125 = (f32[256]{0:T(256)S(1)}, f32[256]{0:T(256)S(1)}, f32[256]{0:T(256)S(1)}, f32[256]{0:T(256)S(1)}, f32[256]{0:T(256)S(1)}, /*index=5...) fusion(f32[256]{0:T(256)S(1)} %bitcast.1222, ...), kind=kLoop, calls=%fused_computation.37.clone.1 | loop fusion | flops 24576 | bytes 66816 | tf_op jit(solution)/shard_map/while/body/eval_jaxpr/div | solution.py:42
  392.7 19.7 %subtract_divide_fusion.125 = (f32[256]{0:T(256)S(1)}, f32[256]{0:T(256)S(1)}, f32[256]{0:T(256)S(1)}, f32[256]{0:T(256)S(1)}, f32[256]{0:T(256)S(1)}, /*index=5...) fusion(f32[256]{0:T(256)S(1)} %bitcast.1222, ...), kind=kLoop, calls=%fused_computation.37.clone.1 | loop fusion | flops 24576 | bytes 66816 | tf_op jit(solution)/shard_map/while/body/eval_jaxpr/div | solution.py:42
  456.5 19.7 %subtract_divide_fusion.125 = (f32[256]{0:T(256)S(1)}, f32[256]{0:T(256)S(1)}, f32[256]{0:T(256)S(1)}, f32[256]{0:T(256)S(1)}, f32[256]{0:T(256)S(1)}, /*index=5...) fusion(f32[256]{0:T(256)S(1)} %bitcast.1222, ...), kind=kLoop, calls=%fused_computation.37.clone.1 | loop fusion | flops 24576 | bytes 66816 | tf_op jit(solution)/shard_map/while/body/eval_jaxpr/div | solution.py:42
  518.1 19.1 %subtract_divide_fusion.32 = (f32[256]{0:T(256)S(1)}, f32[256]{0:T(256)S(1)}, f32[256]{0:T(256)S(1)}, f32[256]{0:T(256)S(1)}, f32[256]{0:T(256)S(1)}, /*index=5*...) fusion(f32[256]{0:T(256)S(1)} %bitcast.1441, ...), kind=kLoop, calls=%fused_computation.321 | loop fusion | flops 23808 | bytes 64760 | tf_op jit(solution)/shard_map/eval_jaxpr/div | solution.py:42
  539.8 151.9 %while.9 = (s32[]{:T(128)}, f32[256]{0:T(256)S(1)}, f32[7,32,256]{2,1,0:T(8,128)S(1)}, f32[7,32,256]{2,1,0:T(8,128)S(1)}, f32[7,32]{1,0:T(8,128)S(1)}, /*index=5...) while((s32[]{:T(128)}, f32[256]{0:T(256)S(1)}, ...), condition=%wide.region_3.4_spmd, body=%wide.region_2.3_spmd.sunk | while | flops 16418 | bytes 266721 | solution.py:42
  541.4 19.9 %multiply_subtract_fusion.125 = (f32[256]{0:T(256)S(1)}, f32[256]{0:T(256)S(1)}, f32[256]{0:T(256)S(1)}, f32[256]{0:T(256)S(1)}, f32[256]{0:T(256)S(1)}, /*index...) fusion(f32[256]{0:T(256)S(1)} %bitcast.1289, ...), kind=kLoop, calls=%fused_computation.103.clone.1 | loop fusion | flops 16384 | bytes 66688 | tf_op jit(solution)/shard_map/while/body/eval_jaxpr/sub | solution.py:42
  563.1 19.9 %multiply_subtract_fusion.125 = (f32[256]{0:T(256)S(1)}, f32[256]{0:T(256)S(1)}, f32[256]{0:T(256)S(1)}, f32[256]{0:T(256)S(1)}, f32[256]{0:T(256)S(1)}, /*index...) fusion(f32[256]{0:T(256)S(1)} %bitcast.1289, ...), kind=kLoop, calls=%fused_computation.103.clone.1 | loop fusion | flops 16384 | bytes 66688 | tf_op jit(solution)/shard_map/while/body/eval_jaxpr/sub | solution.py:42
  584.8 19.9 %multiply_subtract_fusion.125 = (f32[256]{0:T(256)S(1)}, f32[256]{0:T(256)S(1)}, f32[256]{0:T(256)S(1)}, f32[256]{0:T(256)S(1)}, f32[256]{0:T(256)S(1)}, /*index...) fusion(f32[256]{0:T(256)S(1)} %bitcast.1289, ...), kind=kLoop, calls=%fused_computation.103.clone.1 | loop fusion | flops 16384 | bytes 66688 | tf_op jit(solution)/shard_map/while/body/eval_jaxpr/sub | solution.py:42
  606.6 19.9 %multiply_subtract_fusion.125 = (f32[256]{0:T(256)S(1)}, f32[256]{0:T(256)S(1)}, f32[256]{0:T(256)S(1)}, f32[256]{0:T(256)S(1)}, f32[256]{0:T(256)S(1)}, /*index...) fusion(f32[256]{0:T(256)S(1)} %bitcast.1289, ...), kind=kLoop, calls=%fused_computation.103.clone.1 | loop fusion | flops 16384 | bytes 66688 | tf_op jit(solution)/shard_map/while/body/eval_jaxpr/sub | solution.py:42
  628.3 19.9 %multiply_subtract_fusion.125 = (f32[256]{0:T(256)S(1)}, f32[256]{0:T(256)S(1)}, f32[256]{0:T(256)S(1)}, f32[256]{0:T(256)S(1)}, f32[256]{0:T(256)S(1)}, /*index...) fusion(f32[256]{0:T(256)S(1)} %bitcast.1289, ...), kind=kLoop, calls=%fused_computation.103.clone.1 | loop fusion | flops 16384 | bytes 66688 | tf_op jit(solution)/shard_map/while/body/eval_jaxpr/sub | solution.py:42
  650.0 19.9 %multiply_subtract_fusion.125 = (f32[256]{0:T(256)S(1)}, f32[256]{0:T(256)S(1)}, f32[256]{0:T(256)S(1)}, f32[256]{0:T(256)S(1)}, f32[256]{0:T(256)S(1)}, /*index...) fusion(f32[256]{0:T(256)S(1)} %bitcast.1289, ...), kind=kLoop, calls=%fused_computation.103.clone.1 | loop fusion | flops 16384 | bytes 66688 | tf_op jit(solution)/shard_map/while/body/eval_jaxpr/sub | solution.py:42
  671.7 19.9 %multiply_subtract_fusion.125 = (f32[256]{0:T(256)S(1)}, f32[256]{0:T(256)S(1)}, f32[256]{0:T(256)S(1)}, f32[256]{0:T(256)S(1)}, f32[256]{0:T(256)S(1)}, /*index...) fusion(f32[256]{0:T(256)S(1)} %bitcast.1289, ...), kind=kLoop, calls=%fused_computation.103.clone.1 | loop fusion | flops 16384 | bytes 66688 | tf_op jit(solution)/shard_map/while/body/eval_jaxpr/sub | solution.py:42
  691.7 19.3 %multiply_subtract_fusion.32 = (f32[256]{0:T(256)S(1)}, f32[256]{0:T(256)S(1)}, f32[256]{0:T(256)S(1)}, f32[256]{0:T(256)S(1)}, f32[256]{0:T(256)S(1)}, /*index=...) fusion(f32[256]{0:T(256)S(1)} %bitcast.1387, ...), kind=kLoop, calls=%fused_computation.290 | loop fusion | flops 15872 | bytes 64636 | tf_op jit(solution)/shard_map/eval_jaxpr/sub | solution.py:42
  715.4 11.8 %pad_slice_fusion.21 = (f32[5,256,6,256]{3,1,2,0:T(8,128)}, f32[5,256,6,256]{3,1,2,0:T(8,128)}, f32[5,256,6,256]{3,1,2,0:T(8,128)}, f32[5,256,6,256]{3,1,2,0:T(8,128)}) fusion(f32[5,256,6,256]{3,1,2,0:T(8,128)S(1)} %bitcast.1153), kind=kLoop, calls=%fused_computation.165 | loop fusion | bytes 39321600 | tf_op jit(solution)/shard_map/slice | solution.py:51
  727.1 15.4 %fusion.1 = f32[5,252,6,256]{3,1,2,0:T(8,128)} fusion(f32[5,256,6,256]{3,1,2,0:T(8,128)} %get-tuple-element.519, f32[5,256,6,256]{3,1,2,0:T(8,128)} %get-tuple-element.521, f32[5,256,6,256]{3,1,2,0:T(8,128)} %get-tuple-element.520, f32[5,256,6,256]{3,1,2,0:T(8,128)} %get-tuple-element.518), kind=kLoop, calls=%fused_computation.153 | loop fusion | flops 9676800 | bytes 38707200 | tf_op jit(solution)/shard_map/add | solution.py:56
  742.5 24.6 %concatenate.55 = f32[5,256,6,256]{3,1,2,0:T(8,128)} concatenate(f32[5,1,6,256]{3,1,2,0:T(1,128)S(1)} %get-tuple-element.517, f32[5,1,6,256]{3,1,2,0:T(1,128)S(1)} %get-tuple-element.516, f32[5,252,6,256]{3,1,2,0:T(8,128)} %fusion.1, f32[5,1,6,256]{3,1,2,0:T(1,128)S(1)} %get-tuple-element.515, f32[5,1,6,256]{3,1,2,0:T(1,128)S(1)} %get-tuple-element.514), dimensions={1} | concatenate | bytes 15728640 | tf_op jit(solution)/shard_map/concatenate | solution.py:64
  915.4 35.8 %fusion.8 = f32[3,32,48,256]{3,2,1,0:T(8,128)} fusion(f32[3,32,48,256]{3,1,2,0:T(8,128)} %get-tuple-element.529, f32[3,32,48,256]{3,1,2,0:T(8,128)} %get-tuple-element.526, f32[3,32,48,256]{3,1,2,0:T(8,128)} %get-tuple-element.528, f32[3,32,48,256]{3,1,2,0:T(8,128)} %get-tuple-element.525, f32[3,32,48,256]{3,1,2,0:T(8,128)} %get-tuple-element.527, ...), kind=kLoop, calls=%fused_computation.176 | loop fusion | flops 9437184 | bytes 33030144 | tf_op jit(solution)/shard_map/add | solution.py:73
  968.1 13.1 %fusion.30 = (f32[32,48,256]{2,1,0:T(8,128)S(1)}, f32[32,48,256]{2,1,0:T(8,128)S(1)}, f32[32,48,256]{2,1,0:T(8,128)}, f32[32,48,256]{2,1,0:T(8,128)}) fusion(f32[3,32,48,256]{3,2,1,0:T(8,128)} %fusion.50, f32[3,32,48,256]{3,2,1,0:T(8,128)S(1)} %copy-done.2, f32[32,48,256]{2,1,0:T(8,128)S(1)} %copy-done.5, f32[32,48,256]{2,0,1:T(8,128)S(1)} %bitcast.1164, ...), kind=kLoop, calls=%fused_computation.206 | loop fusion | flops 7864320 | bytes 29884416 | tf_op jit(solution)/shard_map/neg | solution.py:100
  1030.4 134.9 %reduce-scatter.4.cloned.1.call-done = f32[16,64]{1,0:T(8,128)} async-done(((f32[512,64]{1,0:T(8,128)}), f32[16,64]{1,0:T(8,128)}) %reduce-scatter.4.cloned.1.call-update) | async-done | bytes 4112
  (269 shorter events, 282.1 us)
Async XLA Ops:
  11.1 3.1 copy-start
  21.9 689.3 %all-to-all-start = ((f32[5,32,48,256]{3,1,0,2:T(8,128)}), f32[5,32,48,256]{3,1,0,2:T(8,128)}, u32[]{:S(2)}, u32[]{:S(2)}) async-start(f32[5,32,48,256]{3,1,0,2:T(8,128)} %copy.115), calls=%async_computation | async-start | bytes 15728640 | tf_op jit(solution)/shard_map/all_to_all | solution.py:80
  785.6 177.4 %all-to-all-start.1 = ((f32[8,5,32,6,256]{4,2,3,1,0:T(8,128)}), f32[8,5,32,6,256]{4,2,3,1,0:T(8,128)}, u32[]{:S(2)}, u32[]{:S(2)}) async-start(f32[8,5,32,6,256]{4,2,3,1,0:T(8,128)} %fusion.33), calls=%async_computation.1 | async-start | bytes 15728640 | tf_op jit(solution)/shard_map/all_to_all | solution.py:85
  791.6 373.7 %reduce-scatter.4.cloned.1.call-start = ((), (), s32[]{:S(2)}) async-start(), calls=%async_computation.3 | async-start | bytes 270336
  794.3 6.6 copy-start.1
  794.3 6.7 copy-start.4
  795.2 85.1 %collective-permute-start.1 = (f32[3,32,3,256]{3,1,2,0:T(8,128)}, f32[3,32,3,256]{3,1,2,0:T(8,128)}, u32[]{:S(2)}, u32[]{:S(2)}) collective-permute-start(f32[3,32,3,256]{3,1,2,0:T(8,128)} %copy.194), channel_id=1, source_target_pairs={{0,1},{1,2},{2,3},{4,5},{5,6},{6,7},{8,9},{9,10},{10,11},{12,13},{... | collective-permute-start | bytes 884744 | tf_op jit(solution)/shard_map/ppermute | solution.py:17
  798.1 92.7 %collective-permute-start = (f32[3,32,3,256]{3,1,2,0:T(8,128)}, f32[3,32,3,256]{3,1,2,0:T(8,128)}, u32[]{:S(2)}, u32[]{:S(2)}) collective-permute-start(f32[3,32,3,256]{3,1,2,0:T(8,128)} %copy.195), channel_id=1, source_target_pairs={{1,0},{2,1},{3,2},{5,4},{6,5},{7,6},{9,8},{10,9},{11,10},{13,12},{... | collective-permute-start | bytes 884744 | tf_op jit(solution)/shard_map/ppermute | solution.py:20
  800.9 2.2 copy-start.3
  859.0 11.7 copy-start.13
  859.0 11.8 %copy-start.11 = (f32[3,192]{1,0:T(4,128)S(1)}, f32[3,192]{1,0:T(4,128)}, u32[]{:S(2)}) copy-start(f32[3,192]{1,0:T(4,128)} %param.14) | copy-start | bytes 6916
  859.0 11.8 %copy-start.12 = (f32[3,192]{1,0:T(4,128)S(1)}, f32[3,192]{1,0:T(4,128)}, u32[]{:S(2)}) copy-start(f32[3,192]{1,0:T(4,128)} %param.15) | copy-start | bytes 6916
  871.4 8.4 copy-start.10
  962.9 4.7 copy-start.2
  962.9 5.2 copy-start.5
  999.6 2.7 copy-start.6
  1002.3 5.5 copy-start.7
  1002.3 5.5 copy-start.8
  1007.8 14.3 %copy-start.9 = (s32[192,512]{1,0:T(8,128)S(1)}, s32[192,512]{1,0:T(8,128)}, u32[]{:S(2)}) copy-start(s32[192,512]{1,0:T(8,128)} %param.17) | copy-start | bytes 1179652
Sparse Core Ops, SparseCore 0:
  1030.5 134.6 reduce-scatter.3
